TPU v7x, 32 devices: a whole 2x2x4 slice. The times are simulated.
32 devices in a mesh: seq: 16 (over z, y, x), head: 2 (over core).
Axes of the slice: x: 2, y: 2, z: 4, core: 2. Of those that a mesh axis runs over, the one named last changes fastest.
Arguments:
- hidden_state: bfloat16 [8, 4096], replicated, may hold values from -18 to 18
- query_weight: bfloat16 [4096, 2, 2048], P('seq', 'head'), may hold values from -1 to 1
- up_key: bfloat16 [2, 256, 512], P('head'), may hold values from -1 to 1
- up_value: bfloat16 [2, 256, 512], P('head'), may hold values from -0.375 to 0.375
- latent_key: bfloat16 [8, 16384, 2, 256], P(None, 'seq', 'head'), may hold values from -256 to 256
- latent_value: bfloat16 [8, 16384, 2, 256], P(None, 'seq', 'head'), may hold values from -6 to 6
- lengths: int32 [8], replicated, may hold values from 12288 to 16384
- block_mask: int32 [8, 64], P(None, 'seq'), may hold values from 0 to 1, as said below
- out_weight: bfloat16 [2, 2048, 4096], P('head', 'seq'), may hold values from -0.09375 to 0.09375
Outputs:
- attn_out: float32 [8, 4096], replicated
Inputs may be any that keep to these rules, and one draw needn't show every extreme that they name: `block_mask`: blocks 0 and 32 of every sequence are valid.
All inputs are finite; a program needn't handle non-finite values.
Results may differ from a plain program's by a relative error of at most 0.0035.
Values sent between devices are 32-bit elements; how exact they have to be, the bound alone decides.
No kernel may reach another device: no remote copies, remote signals or barrier semaphores. Data moves between devices by JAX's collectives and lax.ppermute only.
A program may use at most 64 MiB of HBM per device.

v0:
```python
import math
import jax
import jax.numpy as jnp
from jax import lax
from jax.sharding import PartitionSpec as P

HD = 128
R = 256
BLOCK = 256
KPG = 4
REP = 4
QW = 2048


def joined(part, axis, combine):
    gathered = jax.tree.map(lambda a: lax.all_gather(a, axis), part)

    def take(source):
        return jax.tree.map(lambda a: lax.dynamic_index_in_dim(a, source, 0, False), gathered)

    return lax.fori_loop(
        1, lax.axis_size(axis), lambda source, state: combine(state, take(source)), take(0)
    )


def join_carries(earlier, later):
    peak_a, total_a, summed_a = earlier
    peak_b, total_b, summed_b = later
    peak = jnp.maximum(peak_a, peak_b)
    factor_a = jnp.exp(peak_a - peak)
    factor_b = jnp.exp(peak_b - peak)
    total = total_a * factor_a + total_b * factor_b
    summed = summed_a * factor_a[..., None] + summed_b * factor_b[..., None]
    return (peak, total, summed)


def body(
    hidden_state,
    query_weight,
    up_key,
    up_value,
    latent_key,
    latent_value,
    lengths,
    block_mask,
    out_weight,
):
    highest = lax.Precision.HIGHEST
    seq_index = lax.axis_index("seq")
    batch = hidden_state.shape[0]
    dim_rows = query_weight.shape[0]
    state_rows = lax.dynamic_slice_in_dim(hidden_state, seq_index * dim_rows, dim_rows, 1)
    partial_query = jnp.dot(state_rows, query_weight[:, 0, :], preferred_element_type=jnp.float32)
    query = lax.psum(partial_query, "seq")
    query_heads = query.reshape(batch, KPG, REP, HD)
    keys_lat = latent_key[:, :, 0, :]
    values_lat = latent_value[:, :, 0, :]
    context_len = keys_lat.shape[1]
    positions = seq_index * context_len + jnp.arange(context_len, dtype=jnp.int32)
    block_full = jnp.repeat(block_mask, BLOCK, axis=1)
    valid = (positions[None, :] < lengths[:, None]) & (block_full > 0)
    mask_heads = valid[:, None, None, :]
    scale = 1.0 / math.sqrt(HD)
    key_maps = up_key[0].astype(jnp.float32).reshape(R, KPG, HD)
    query_latent = jnp.einsum("bjrd,ejd->bjre", query_heads, key_maps, precision=highest)
    scores = (
        jnp.einsum("bjre,bce->bjrc", query_latent, keys_lat.astype(jnp.float32), precision=highest)
        * scale
    )
    peak = jnp.max(jnp.where(mask_heads, scores, -1e30), axis=-1)
    weights = jnp.where(mask_heads, jnp.exp(scores - peak[..., None]), 0.0)
    total = jnp.sum(weights, axis=-1)
    value_maps = up_value[0].astype(jnp.float32).reshape(R, KPG, HD)
    latent_sum = jnp.einsum(
        "bjrc,bce->bjre", weights, values_lat.astype(jnp.float32), precision=highest
    )
    summed = jnp.einsum("bjre,ejd->bjrd", latent_sum, value_maps, precision=highest)
    out_rows = out_weight.shape[1]
    peak_all, total_all, summed_all = joined((peak, total, summed), "seq", join_carries)
    context = (summed_all / total_all[..., None]).reshape(batch, QW).astype(jnp.bfloat16)
    context_rows = lax.dynamic_slice_in_dim(context, seq_index * out_rows, out_rows, 1)
    partial_out = jnp.dot(context_rows, out_weight[0], preferred_element_type=jnp.float32)
    return lax.psum(partial_out, ("seq", "head"))


def solution(mesh):
    in_specs = (
        P(),
        P("seq", "head", None),
        P("head", None, None),
        P("head", None, None),
        P(None, "seq", "head", None),
        P(None, "seq", "head", None),
        P(),
        P(None, "seq"),
        P("head", "seq", None),
    )
    out_specs = P()
    return jax.shard_map(body, mesh=mesh, in_specs=in_specs, out_specs=out_specs, check_vma=False)
```

profile of v0, /device:TPU:0, one launch (start us, length us, event | category | flops | bytes accessed | tf_op | source)
XLA Modules:
  0.0 361.0 jit_solution(18013315302296954894)
XLA Ops:
  6.5 1.6 fusion.13
  8.1 0.7 copy.28
  8.8 0.7 broadcast_compare_fusion
  9.6 0.7 compare_and_fusion
  10.3 1.0 reshape.54
  11.4 1.0 reshape.55
  12.4 106.7 %all-reduce.3.cloned.1.call-done = f32[8,4,4,128]{3,2,1,0:T(4,128)} async-done(((f32[8,4,4,128]{3,2,1,0:T(4,128)}), f32[8,4,4,128]{3,2,1,0:T(4,128)}) %all-reduce.3.cloned.1.call-update) | async-done | bytes 65552 | tf_op jit(solution)/shard_map/psum | solution.py:54
  119.1 1.4 convolution_bitcast_fusion
  120.4 5.7 %select_reduce_fusion = (f32[8,4,4]{2,1,0:T(4,128)S(1)}, f32[8,4,4,1024]{3,2,1,0:T(4,128)S(1)}) fusion(pred[8,1024]{1,0:T(8,128)(4,1)S(1)} %compare_and_fusion, f32[8,4,4,256]{3,2,1,0:T(4,128)S(1)} %convolution_bitcast_fusion, bf16[8,1024,1,256]{3,1,2,0:T(8,128)(2,1)} %param.15), kind=kOutput, calls=%fused_computation.22 | convolution fusion | flops 403046272 | bytes 4858368 | tf_op jit(solution)/shard_map/bjre,bce->bjrc/dot_general | solution.py:67
  126.1 2.1 fusion.4
  128.2 0.9 convolution_bitcast_fusion.1
  129.2 40.4 %all-gather = f32[128,4,4]{2,1,0:T(4,128)S(1)} all-gather(f32[8,4,4]{2,1,0:T(4,128)S(1)} %get-tuple-element.223), channel_id=2, replica_groups=mesh['seq'=16,'head'=2] {'seq'}, dimensions={0}, use_global_device_ids=true | all-gather | bytes 8704 | tf_op jit(solution)/shard_map/all_gather | solution.py:16
  169.7 0.1 copy.34
  169.8 0.5 copy.37
  170.2 0.4 fusion.15
  170.6 37.1 %all-gather.1 = f32[128,4,4]{2,1,0:T(4,128)S(1)} all-gather(f32[8,4,4]{2,1,0:T(4,128)S(1)} %fusion.15), channel_id=3, replica_groups=mesh['seq'=16,'head'=2] {'seq'}, dimensions={0}, use_global_device_ids=true | all-gather | bytes 8704 | tf_op jit(solution)/shard_map/all_gather | solution.py:16
  207.8 0.1 copy.35
  207.9 0.5 copy.38
  208.4 0.8 slice.8
  209.2 20.1 %while.19 = (s32[]{:T(128)}, f32[8,4,4]{0,2,1:T(4,128)S(1)}, f32[8,4,4]{0,2,1:T(4,128)S(1)}, f32[8,4,4,128]{3,2,1,0:T(4,128)S(1)}, f32[16,8,4,4]{1,3,2,0:T(4,128...) while((s32[]{:T(128)}, f32[8,4,4]{0,2,1:T(4,128)S(1)}, ...), condition=%wide.region_4.5_spmd, body=%wide.region_3.4_spmd.sunk | while | flops 49925 | bytes 334991 | solution.py:21
  209.3 0.1 copy.68
  209.5 0.8 constant_dynamic-slice_fusion.2
  210.3 0.2 fusion.34
  210.6 0.1 copy.68
  210.8 0.8 constant_dynamic-slice_fusion.2
  211.7 0.2 fusion.34
  212.0 0.1 copy.68
  212.2 0.8 constant_dynamic-slice_fusion.2
  213.0 0.2 fusion.34
  213.3 0.1 copy.68
  213.5 0.8 constant_dynamic-slice_fusion.2
  214.4 0.2 fusion.34
  214.6 0.1 copy.68
  214.9 0.8 constant_dynamic-slice_fusion.2
  215.7 0.2 fusion.34
  216.0 0.1 copy.68
  216.2 0.8 constant_dynamic-slice_fusion.2
  217.0 0.2 fusion.34
  217.3 0.1 copy.68
  217.5 0.8 constant_dynamic-slice_fusion.2
  218.4 0.2 fusion.34
  218.7 0.1 copy.68
  218.9 0.8 constant_dynamic-slice_fusion.2
  219.7 0.2 fusion.34
  220.0 0.1 copy.68
  220.2 0.8 constant_dynamic-slice_fusion.2
  221.1 0.2 fusion.34
  221.5 0.8 constant_dynamic-slice_fusion.2
  222.4 0.2 fusion.34
  222.9 0.8 constant_dynamic-slice_fusion.2
  223.7 0.2 fusion.34
  224.2 0.8 constant_dynamic-slice_fusion.2
  225.1 0.2 fusion.34
  225.6 0.8 constant_dynamic-slice_fusion.2
  226.4 0.2 fusion.34
  226.9 0.8 constant_dynamic-slice_fusion.2
  227.8 0.2 fusion.34
  228.2 0.8 constant_dynamic-slice_fusion.2
  229.1 0.2 fusion.34
  229.3 0.1 copy.40
  229.4 0.1 divide_convert_fusion
  229.6 0.9 fusion.11
  230.5 122.4 %all-reduce.5.cloned.1.call-done = f32[8,4096]{1,0:T(8,128)} async-done(((f32[8,4096]{1,0:T(8,128)}), f32[8,4096]{1,0:T(8,128)}) %all-reduce.5.cloned.1.call-update) | async-done | bytes 131088 | tf_op jit(solution)/shard_map/psum | solution.py:83
  352.9 1.6 copy.84
  (53 shorter events, 2.9 us)
Async XLA Ops:
  6.5 223.1 %copy-start = (bf16[1,128,4096]{2,1,0:T(8,128)(2,1)S(1)}, bf16[1,128,4096]{2,1,0:T(8,128)(2,1)}, u32[]{:S(2)}) copy-start(bf16[1,128,4096]{2,1,0:T(8,128)(2,1)} %param.19) | copy-start | bytes 3145732
  6.5 112.5 %all-reduce.3.cloned.1.call-start = ((), (), s32[]{:S(2)}) async-start(), calls=%async_computation | async-start | bytes 131072 | tf_op jit(solution)/shard_map/psum | solution.py:54
  8.8 199.6 %all-gather.5.cloned.1.call-start = ((), (), s32[]{:S(2)}) async-start(), calls=%async_computation.2 | async-start | bytes 1114112 | tf_op jit(solution)/shard_map/all_gather | solution.py:16
  119.1 7.0 %copy-start.1 = (bf16[8,1024,1,256]{3,1,2,0:T(8,128)(2,1)S(1)}, bf16[8,1024,1,256]{3,1,2,0:T(8,128)(2,1)}, u32[]{:S(2)}) copy-start(bf16[8,1024,1,256]{3,1,2,0:T(8,128)(2,1)} %param.16) | copy-start | bytes 12582916
  129.2 223.8 %all-reduce.5.cloned.1.call-start = ((), (), s32[]{:S(2)}) async-start(), calls=%async_computation.1 | async-start | bytes 262144 | tf_op jit(solution)/shard_map/psum | solution.py:83
Sparse Core Ops, SparseCore 0:
  12.8 106.2 all-reduce.2
  129.3 55.2 all-gather.4
  230.7 122.2 all-reduce.4
where the time goes:
time: 362 us; the launch traced here: 361 us
  waiting for transfers between devices  229 us (63%)
  blocking collectives  77.6 us (21%)
  local copies, waits for them, and re-layouts  22.3 us (6%)
  between operations  13.2 us (4%)
  matrix products  12.6 us (3%)
  other arithmetic  5.93 us (2%)
    psum x1, waiting for transfers between devices, body(): return lax.psum(partial_out, ('seq', 'head'))  122 us
    psum x1, waiting for transfers between devices, body(): query = lax.psum(partial_query, 'seq')  107 us
    all_gather x2, blocking collectives, joined(): gathered = jax.tree.map(lambda a: lax.all_gather(a, axis), part)  77.6 us
    dynamic_slice x18, local copies, waits for them, and re-layouts, take(): lax.dynamic_index_in_dim(a, source, 0, False)  13.5 us
  transfers between devices with their start and end apart: 3, of which 2 were waited for; matrix products, arithmetic and copies ran while one was open for 1% of the time, Pallas kernels for 0%

commit v1 on v0

--- a/solution.py
+++ b/solution.py
@@ -51,7 +51,9 @@
     dim_rows = query_weight.shape[0]
     state_rows = lax.dynamic_slice_in_dim(hidden_state, seq_index * dim_rows, dim_rows, 1)
     partial_query = jnp.dot(state_rows, query_weight[:, 0, :], preferred_element_type=jnp.float32)
-    query = lax.psum(partial_query, "seq")
+    query = partial_query
+    for hop in (1, 2, 4, 8):
+        query = query + lax.ppermute(query, "seq", [(dev, dev ^ hop) for dev in range(16)])
     query_heads = query.reshape(batch, KPG, REP, HD)
     keys_lat = latent_key[:, :, 0, :]
     values_lat = latent_value[:, :, 0, :]

time: 362 us -> 273 us (0.75)
  waiting for transfers between devices: 229 us -> 128 us
  starting transfers between devices: 0.09 us -> 10.7 us
    psum x1 -> x0, waiting for transfers between devices: 107 us -> none  [body(): query = lax.psum(partial_query, 'seq')]
    ppermute x0 -> x4, starting transfers between devices: none -> 10.7 us  [body(): lax.ppermute(query, 'seq', [(dev, dev ^ hop) for dev in range(16)])]
    ppermute x0 -> x4, waiting for transfers between devices: none -> 6.05 us  [body(): lax.ppermute(query, 'seq', [(dev, dev ^ hop) for dev in range(16)])]
  transfers between devices with their start and end apart: 3 -> 6, of which waited for: 2 -> 4; matrix products, arithmetic and copies ran while one was open for 1% -> 2% of each run, Pallas kernels for 0% -> 0%
where the time goes in v1:
time: 273 us; the launch traced here: 272 us
  waiting for transfers between devices  128 us (47%)
  blocking collectives  79.8 us (29%)
  local copies, waits for them, and re-layouts  21.6 us (8%)
  between operations  13.5 us (5%)
  matrix products  11.8 us (4%)
  starting transfers between devices  10.7 us (4%)
  other arithmetic  5.96 us (2%)
    psum x1, waiting for transfers between devices, body(): return lax.psum(partial_out, ('seq', 'head'))  122 us
    all_gather x2, blocking collectives, joined(): gathered = jax.tree.map(lambda a: lax.all_gather(a, axis), part)  79.8 us
    dynamic_slice x18, local copies, waits for them, and re-layouts, take(): lax.dynamic_index_in_dim(a, source, 0, False)  13.5 us
    ppermute x4, starting transfers between devices, body(): lax.ppermute(query, 'seq', [(dev, dev ^ hop) for dev in range(16)])  10.7 us
    ppermute x4, waiting for transfers between devices, body(): lax.ppermute(query, 'seq', [(dev, dev ^ hop) for dev in range(16)])  6.05 us
    dot_general x1, matrix products, body(): jnp.einsum('bjre,bce->bjrc', query_latent, keys_lat.astype(jnp.float32),...  5.88 us
  transfers between devices with their start and end apart: 6, of which 4 were waited for; matrix products, arithmetic and copies ran while one was open for 2% of the time, Pallas kernels for 0%

profile of v1, /device:TPU:0, one launch (start us, length us, event | category | flops | bytes accessed | tf_op | source)
XLA Modules:
  0.0 271.7 jit_solution(16732586622730276703)
XLA Ops:
  6.5 1.6 fusion.13
  8.1 3.0 %collective-permute-start = (f32[8,2048]{1,0:T(8,128)S(1)}, f32[8,2048]{1,0:T(8,128)S(1)}, u32[]{:S(2)}, u32[]{:S(2)}) collective-permute-start(f32[8,2048]{1,0:T(8,128)S(1)} %fusion.13), channel_id=1, source_target_pairs={{0,2},{2,0},{4,6},{6,4},{8,10},{10,8},{12,14},{14,12},{16,18},{18,... | collective-permute-start | bytes 196616 | tf_op jit(solution)/shard_map/ppermute | solution.py:56
  11.1 2.2 collective-permute-done
  13.3 2.1 collective-permute-start.1
  15.5 0.7 broadcast_compare_fusion
  16.1 1.6 collective-permute-done.1
  17.7 2.1 collective-permute-start.2
  19.9 2.2 collective-permute-done.2
  22.1 3.4 %collective-permute-start.3 = (f32[8,2048]{1,0:T(8,128)S(1)}, f32[8,2048]{1,0:T(8,128)S(1)}, u32[]{:S(2)}, u32[]{:S(2)}) collective-permute-start(f32[8,2048]{1,0:T(8,128)S(1)} %add.95), channel_id=1, source_target_pairs={{0,16},{2,18},{4,20},{6,22},{8,24},{10,26},{12,28},{14,30},{16,0},... | collective-permute-start | bytes 196616 | tf_op jit(solution)/shard_map/ppermute | solution.py:56
  25.6 0.7 compare_and_fusion
  26.4 1.0 reshape.54
  27.4 1.0 reshape.55
  28.5 0.4 convolution_bitcast_fusion
  28.8 5.9 %select_reduce_fusion = (f32[8,4,4]{2,1,0:T(4,128)S(1)}, f32[8,4,4,1024]{3,2,1,0:T(4,128)S(1)}) fusion(pred[8,1024]{1,0:T(8,128)(4,1)S(1)} %compare_and_fusion, f32[8,4,4,256]{3,2,1,0:T(4,128)S(1)} %convolution_bitcast_fusion, bf16[8,1024,1,256]{3,1,2,0:T(8,128)(2,1)} %param.15), kind=kOutput, calls=%fused_computation.22 | convolution fusion | flops 403046272 | bytes 4858368 | tf_op jit(solution)/shard_map/bjre,bce->bjrc/dot_general | solution.py:69
  34.7 2.1 fusion.4
  36.8 0.9 convolution_bitcast_fusion.1
  37.8 42.4 %all-gather = f32[128,4,4]{2,1,0:T(4,128)S(1)} all-gather(f32[8,4,4]{2,1,0:T(4,128)S(1)} %get-tuple-element.223), channel_id=2, replica_groups=mesh['seq'=16,'head'=2] {'seq'}, dimensions={0}, use_global_device_ids=true | all-gather | bytes 8704 | tf_op jit(solution)/shard_map/all_gather | solution.py:16
  80.2 0.1 copy.34
  80.3 0.5 copy.37
  80.8 0.4 fusion.15
  81.2 37.4 %all-gather.1 = f32[128,4,4]{2,1,0:T(4,128)S(1)} all-gather(f32[8,4,4]{2,1,0:T(4,128)S(1)} %fusion.15), channel_id=3, replica_groups=mesh['seq'=16,'head'=2] {'seq'}, dimensions={0}, use_global_device_ids=true | all-gather | bytes 8704 | tf_op jit(solution)/shard_map/all_gather | solution.py:16
  118.6 0.1 copy.35
  118.7 0.5 copy.38
  119.2 0.8 slice.8
  120.0 20.1 %while.19 = (s32[]{:T(128)}, f32[8,4,4]{0,2,1:T(4,128)S(1)}, f32[8,4,4]{0,2,1:T(4,128)S(1)}, f32[8,4,4,128]{3,2,1,0:T(4,128)S(1)}, f32[16,8,4,4]{1,3,2,0:T(4,128...) while((s32[]{:T(128)}, f32[8,4,4]{0,2,1:T(4,128)S(1)}, ...), condition=%wide.region_3.4_spmd, body=%wide.region_2.3_spmd.sunk | while | flops 49925 | bytes 334991 | solution.py:21
  120.1 0.1 copy.70
  120.3 0.8 constant_dynamic-slice_fusion.2
  121.1 0.2 fusion.34
  121.4 0.1 copy.70
  121.6 0.8 constant_dynamic-slice_fusion.2
  122.5 0.2 fusion.34
  122.8 0.1 copy.70
  123.0 0.8 constant_dynamic-slice_fusion.2
  123.8 0.2 fusion.34
  124.1 0.1 copy.70
  124.3 0.8 constant_dynamic-slice_fusion.2
  125.2 0.2 fusion.34
  125.7 0.8 constant_dynamic-slice_fusion.2
  126.5 0.2 fusion.34
  127.0 0.8 constant_dynamic-slice_fusion.2
  127.8 0.2 fusion.34
  128.1 0.1 copy.70
  128.3 0.8 constant_dynamic-slice_fusion.2
  129.2 0.2 fusion.34
  129.7 0.8 constant_dynamic-slice_fusion.2
  130.5 0.2 fusion.34
  131.0 0.8 constant_dynamic-slice_fusion.2
  131.9 0.2 fusion.34
  132.3 0.8 constant_dynamic-slice_fusion.2
  133.2 0.2 fusion.34
  133.7 0.8 constant_dynamic-slice_fusion.2
  134.5 0.2 fusion.34
  135.0 0.8 constant_dynamic-slice_fusion.2
  135.9 0.2 fusion.34
  136.4 0.8 constant_dynamic-slice_fusion.2
  137.2 0.2 fusion.34
  137.7 0.8 constant_dynamic-slice_fusion.2
  138.6 0.2 fusion.34
  139.0 0.8 constant_dynamic-slice_fusion.2
  139.9 0.2 fusion.34
  140.2 0.1 divide_convert_fusion
  140.4 0.9 fusion.11
  141.3 122.0 %all-reduce.2.cloned.1.call-done = f32[8,4096]{1,0:T(8,128)} async-done(((f32[8,4096]{1,0:T(8,128)}), f32[8,4096]{1,0:T(8,128)}) %all-reduce.2.cloned.1.call-update) | async-done | bytes 131088 | tf_op jit(solution)/shard_map/psum | solution.py:85
  263.3 1.6 copy.85
  (61 shorter events, 3.4 us)
Async XLA Ops:
  6.5 133.9 %copy-start = (bf16[1,128,4096]{2,1,0:T(8,128)(2,1)S(1)}, bf16[1,128,4096]{2,1,0:T(8,128)(2,1)}, u32[]{:S(2)}) copy-start(bf16[1,128,4096]{2,1,0:T(8,128)(2,1)} %param.19) | copy-start | bytes 3145732
  6.5 112.6 %all-gather.5.cloned.1.call-start = ((), (), s32[]{:S(2)}) async-start(), calls=%async_computation.1 | async-start | bytes 1114112 | tf_op jit(solution)/shard_map/all_gather | solution.py:16
  8.1 5.2 %collective-permute-start = (f32[8,2048]{1,0:T(8,128)S(1)}, f32[8,2048]{1,0:T(8,128)S(1)}, u32[]{:S(2)}, u32[]{:S(2)}) collective-permute-start(f32[8,2048]{1,0:T(8,128)S(1)} %fusion.13), channel_id=1, source_target_pairs={{0,2},{2,0},{4,6},{6,4},{8,10},{10,8},{12,14},{14,12},{16,18},{18,... | collective-permute-start | bytes 196616 | tf_op jit(solution)/shard_map/ppermute | solution.py:56
  13.3 4.4 %collective-permute-start.1 = (f32[8,2048]{1,0:T(8,128)S(1)}, f32[8,2048]{1,0:T(8,128)S(1)}, u32[]{:S(2)}, u32[]{:S(2)}) collective-permute-start(f32[8,2048]{1,0:T(8,128)S(1)} %add.93), channel_id=1, source_target_pairs={{0,4},{2,6},{4,0},{6,2},{8,12},{10,14},{12,8},{14,10},{16,20},{18,... | collective-permute-start | bytes 196616 | tf_op jit(solution)/shard_map/ppermute | solution.py:56
  17.7 4.4 %collective-permute-start.2 = (f32[8,2048]{1,0:T(8,128)S(1)}, f32[8,2048]{1,0:T(8,128)S(1)}, u32[]{:S(2)}, u32[]{:S(2)}) collective-permute-start(f32[8,2048]{1,0:T(8,128)S(1)} %add.94), channel_id=1, source_target_pairs={{0,8},{2,10},{4,12},{6,14},{8,0},{10,2},{12,4},{14,6},{16,24},{18,... | collective-permute-start | bytes 196616 | tf_op jit(solution)/shard_map/ppermute | solution.py:56
  22.1 6.3 %collective-permute-start.3 = (f32[8,2048]{1,0:T(8,128)S(1)}, f32[8,2048]{1,0:T(8,128)S(1)}, u32[]{:S(2)}, u32[]{:S(2)}) collective-permute-start(f32[8,2048]{1,0:T(8,128)S(1)} %add.95), channel_id=1, source_target_pairs={{0,16},{2,18},{4,20},{6,22},{8,24},{10,26},{12,28},{14,30},{16,0},... | collective-permute-start | bytes 196616 | tf_op jit(solution)/shard_map/ppermute | solution.py:56
  28.4 6.3 %copy-start.1 = (bf16[8,1024,1,256]{3,1,2,0:T(8,128)(2,1)S(1)}, bf16[8,1024,1,256]{3,1,2,0:T(8,128)(2,1)}, u32[]{:S(2)}) copy-start(bf16[8,1024,1,256]{3,1,2,0:T(8,128)(2,1)} %param.16) | copy-start | bytes 12582916
  37.8 225.5 %all-reduce.2.cloned.1.call-start = ((), (), s32[]{:S(2)}) async-start(), calls=%async_computation | async-start | bytes 262144 | tf_op jit(solution)/shard_map/psum | solution.py:85
Sparse Core Ops, SparseCore 0:
  37.9 56.6 all-gather.4
  141.5 121.7 all-reduce.1
